TPU v7x, 256 devices: a whole 4x4x8 slice. The times are simulated.
256 devices in a mesh: dp: 64 (over y, z, core), mp: 4 (over x).
Axes of the slice: x: 4, y: 4, z: 8, core: 2. Of those that a mesh axis runs over, the one named last changes fastest.
Arguments:
- queries: bfloat16 [196608, 2048], P('dp', 'mp'), may hold values from -30 to 30
- keys: bfloat16 [196608, 512], P('dp', 'mp'), may hold values from -30 to 30
- values: bfloat16 [196608, 512], P('dp', 'mp'), may hold values from -6 to 6
- doc_ids: int32 [196608], P('dp'), may hold values from -1 to 127, as said below
- live_counts: int32 [64], P('dp'), may hold values from 1 to 24, 1408 in all
- out_weight: bfloat16 [2048, 4096], P('dp', 'mp'), may hold values from -0.125 to 0.125
Outputs:
- mixed: bfloat16 [180224, 4096], P('dp', 'mp')
Inputs may be any that keep to these rules, and one draw needn't show every extreme that they name: `live_counts`: each device has 1 to 24 live blocks, 1408 in all, and some device has exactly 24. `doc_ids`: within each block the numbers start at 0 and never fall along the block, and the -1 entries, if any, form the block's tail.
All inputs are finite; a program needn't handle non-finite values.
Results may differ from a plain program's by a relative error of at most 0.0049.
Values may be sent and summed in bfloat16 or wider, within the bound.
No kernel may reach another device: no remote copies, remote signals or barrier semaphores. Data moves between devices by JAX's collectives and lax.ppermute only.
A program may use at most 128 MiB of HBM per device.

v0:
```python
import math
import jax
import jax.numpy as jnp
from jax import lax
from jax.sharding import PartitionSpec as P

HEAD_SIZE = 128
BLOCK = 128
NB = 24
masked_score = -1e30


def from_everyone(shard, axis):
    size = lax.axis_size(axis)
    return lax.all_to_all(
        jnp.broadcast_to(shard[None], (size, *shard.shape)), axis, 0, 0, tiled=True
    )


def in_order(pieces, dim):
    shape = list(pieces.shape[1:])
    shape[dim] *= pieces.shape[0]
    return jnp.moveaxis(pieces, 0, dim).reshape(shape)


def gather_directly(shard, axis, dim):
    pieces = from_everyone(shard, axis)
    return in_order(pieces, dim)


def group_size():
    return 4


def attend_group(operands):
    query_blocks, key_blocks, value_blocks, id_blocks = operands
    number = query_blocks.shape[0]
    query_heads = query_blocks.shape[2] // HEAD_SIZE
    key_heads = key_blocks.shape[2] // HEAD_SIZE
    repeat = query_heads // key_heads
    query_four = query_blocks.reshape(number, BLOCK, key_heads, repeat, HEAD_SIZE)
    key_four = key_blocks.reshape(number, BLOCK, key_heads, HEAD_SIZE)
    value_four = value_blocks.reshape(number, BLOCK, key_heads, HEAD_SIZE)
    scores = jnp.einsum(
        "bihrd,bjhd->bhrij", query_four, key_four, preferred_element_type=jnp.float32
    ) / math.sqrt(HEAD_SIZE)
    places = jnp.arange(BLOCK, dtype=jnp.int32)
    causal = places[None, :] <= places[:, None]
    allowed = (id_blocks[:, :, None] == id_blocks[:, None, :]) & causal[None]
    scores = jnp.where(allowed[:, None, None], scores, masked_score)
    highest = jnp.max(scores, axis=-1, keepdims=True)
    weights = jnp.where(allowed[:, None, None], jnp.exp(scores - highest), 0.0)
    total_counts = jnp.sum(weights, axis=-1)
    summed = jnp.einsum(
        "bhrij,bjhd->bihrd",
        weights.astype(jnp.bfloat16),
        value_four,
        preferred_element_type=jnp.float32,
    )
    summed = summed / jnp.transpose(total_counts, (0, 3, 1, 2))[..., None]
    summed = jnp.where(id_blocks[:, :, None, None, None] >= 0, summed, 0.0)
    return summed.reshape(number, BLOCK, query_heads * HEAD_SIZE).astype(jnp.bfloat16)


def attend_blocks(query_blocks, key_blocks, value_blocks, id_blocks):
    number = query_blocks.shape[0]
    grouping = group_size()

    def regroup(tensor):
        return tensor.reshape((number // grouping, grouping) + tensor.shape[1:])

    result = lax.map(
        attend_group,
        (regroup(query_blocks), regroup(key_blocks), regroup(value_blocks), regroup(id_blocks)),
    )
    return result.reshape((number,) + result.shape[2:])


def locate(labels, targets):
    slots = jnp.arange(labels.shape[0], dtype=jnp.int32)
    hits = labels[None, :] == targets[:, None]
    return jnp.sum(jnp.where(hits, slots[None, :], 0), axis=1)


def body(queries, keys, values, doc_ids, live_counts, out_weight):
    member_list = lax.axis_size("dp")
    per_owner = (NB + member_list - 1) // member_list
    kept_blocks = NB * 11 // 12
    own_index = lax.axis_index("dp")
    live_blocks = live_counts[0]
    full_weight = lax.all_gather(out_weight, "dp", axis=0, tiled=True)
    table = gather_directly(live_counts, "dp", 0)
    first_label = jnp.sum(jnp.where(jnp.arange(member_list, dtype=jnp.int32) < own_index, table, 0))
    owners = jnp.arange(member_list, dtype=jnp.int32)[:, None]
    layers = jnp.arange(per_owner, dtype=jnp.int32)[None, :]
    chosen = ((owners - first_label) % member_list + layers * member_list).reshape(-1)
    usable = chosen < live_blocks
    labels = jnp.where(usable, first_label + chosen, -1)
    chosen = jnp.where(usable, chosen, 0)
    query_cols = queries.shape[1]
    query_blocks = queries.reshape(NB, BLOCK, query_cols)
    key_blocks = keys.reshape(NB, BLOCK, keys.shape[1])
    value_blocks = values.reshape(NB, BLOCK, values.shape[1])
    id_blocks = doc_ids.reshape(NB, BLOCK)
    targets = own_index + jnp.arange(kept_blocks, dtype=jnp.int32) * member_list
    own_result = attend_blocks(query_blocks, key_blocks, value_blocks, id_blocks)
    arrived = (
        lax.all_to_all(own_result[chosen], "dp", split_axis=0, concat_axis=0, tiled=True),
        lax.all_to_all(labels, "dp", split_axis=0, concat_axis=0, tiled=True),
    )
    source = locate(arrived[1], targets)
    attended = arrived[0][source]
    flattened = attended.reshape(kept_blocks * BLOCK, query_cols)
    mixed = jnp.dot(
        lax.all_gather(flattened, "mp", axis=1, tiled=True),
        full_weight,
        preferred_element_type=jnp.float32,
    )
    return mixed.astype(jnp.bfloat16)


def solution(mesh):
    return jax.shard_map(
        body,
        mesh=mesh,
        in_specs=(P("dp", "mp"), P("dp", "mp"), P("dp", "mp"), P("dp"), P("dp"), P("dp", "mp")),
        out_specs=P("dp", "mp"),
        check_vma=False,
    )
```

profile of v0, /device:TPU:1, one launch (start us, length us, event | category | flops | bytes accessed | tf_op | source)
XLA Modules:
  0.0 426.4 jit_solution(5800160574564493758)
XLA Ops:
  7.8 13.1 %all-to-all-start = ((s32[64,1,1]{2,1,0:T(1,128)}), s32[64,1,1]{2,1,0:T(1,128)S(1)}, u32[]{:S(2)}, u32[]{:S(2)}) async-start(s32[64,1,1]{2,1,0:T(1,128)} %broadcast_in_dim.83), calls=%async_computation | async-start | bytes 65536 | tf_op jit(solution)/shard_map/all_to_all | solution.py:15
  21.0 35.9 %while.10 = (s32[]{:T(128)}, bf16[6,4,128,512]{3,2,1,0:T(8,128)(2,1)}, s32[6,4,128]{2,1,0:T(4,128)}, bf16[6,4,128,128]{3,2,1,0:T(8,128)(2,1)}, bf16[6,4,128,128]...) while((s32[]{:T(128)}, bf16[6,4,128,512]{3,2,1,0:T(8,128)(2,1)}, s32[6,4,128]{2,1,0:T(4,128)}, ...), condition=%wide.region_3.4_spmd, body=%wide.region_0.3_spmd.sunk | while | flops 137507328 | bytes 8993897 | solution.py:72
  21.8 1.1 constant_dynamic-slice_fusion.2
  23.2 1.2 fusion.33
  24.7 1.3 select_convert_fusion.2
  26.1 0.8 constant_dynamic-update-slice_fusion.2
  27.8 1.1 constant_dynamic-slice_fusion.2
  29.2 1.2 fusion.33
  30.6 1.3 select_convert_fusion.2
  33.8 1.1 constant_dynamic-slice_fusion.2
  35.2 1.2 fusion.33
  36.6 1.3 select_convert_fusion.2
  39.8 1.1 constant_dynamic-slice_fusion.2
  41.2 1.2 fusion.33
  42.6 1.3 select_convert_fusion.2
  45.8 1.1 constant_dynamic-slice_fusion.2
  47.2 1.2 fusion.33
  48.6 1.3 select_convert_fusion.2
  51.8 1.1 constant_dynamic-slice_fusion.2
  53.1 1.2 fusion.33
  54.6 1.3 select_convert_fusion.2
  56.9 1.2 reduce.2
  59.6 1.4 compare_select_fusion.2
  61.0 10.3 %all-to-all-start.2 = ((s32[64,1,1]{2,1,0:T(1,128)}), s32[64,1,1]{2,1,0:T(1,128)S(1)}, u32[]{:S(2)}, u32[]{:S(2)}) async-start(s32[64,1,1]{2,1,0:T(1,128)} %compare_select_fusion.2), calls=%async_computation.2 | async-start | bytes 65536 | tf_op jit(solution)/shard_map/all_to_all | solution.py:109
  71.3 7.3 %gather_fusion = bf16[64,128,512]{2,1,0:T(8,128)(2,1)} fusion(bf16[24,128,512]{2,1,0:T(8,128)(2,1)} %bitcast.76, s32[1024]{0:T(1024)S(1)} %pad_clamp_fusion.1), kind=kCustom, calls=%fused_computation | custom fusion | bytes 16777472 | tf_op jit(solution)/shard_map/gather | solution.py:108
  78.7 2.0 all-to-all-done.2
  80.6 8.5 %all-to-all-start.1 = ((bf16[64,128,512]{2,1,0:T(8,128)(2,1)}), bf16[64,128,512]{2,1,0:T(8,128)(2,1)}, u32[]{:S(2)}, u32[]{:S(2)}) async-start(bf16[64,128,512]{2,1,0:T(8,128)(2,1)} %gather_fusion), calls=%async_computation.1 | async-start | bytes 16777216 | tf_op jit(solution)/shard_map/all_to_all | solution.py:108
  90.1 1.2 reduce.3
  91.5 195.6 %all-to-all-done.1 = bf16[64,128,512]{2,1,0:T(8,128)(2,1)} async-done(((bf16[64,128,512]{2,1,0:T(8,128)(2,1)}), bf16[64,128,512]{2,1,0:T(8,128)(2,1)}, u32[]{:S(2)}, u32[]{:S(2)}) %all-to-all-start.1) | async-done | bytes 8388640 | tf_op jit(solution)/shard_map/all_to_all | solution.py:108
  287.1 5.8 %gather_fusion.1 = bf16[22,128,512]{2,1,0:T(8,128)(2,1)} fusion(bf16[64,128,512]{2,1,0:T(8,128)(2,1)} %all-to-all-done.1, s32[1024]{0:T(1024)S(1)} %pad_clamp_fusion), kind=kCustom, calls=%fused_computation.1 | custom fusion | bytes 5767256 | tf_op jit(solution)/shard_map/gather | solution.py:112
  293.0 108.8 %all-gather.3.cloned.1.call-done = bf16[2816,2048]{1,0:T(8,128)(2,1)} async-done(((bf16[2816,512]{1,0:T(8,128)(2,1)}), bf16[2816,2048]{1,0:T(8,128)(2,1)}) %all-gather.3.cloned.1.call-update) | async-done | bytes 11534352 | tf_op jit(solution)/shard_map/all_gather | solution.py:115
  401.8 17.8 %convolution_convert_fusion = bf16[2816,1024]{1,0:T(8,128)(2,1)} fusion(bf16[2816,2048]{1,0:T(8,128)(2,1)} %all-gather.3.cloned.1.call-done, bf16[2048,1024]{1,0:T(8,128)(2,1)} %all-gather.5.cloned.1.call-done), kind=kOutput, calls=%fused_computation.27 | convolution fusion | flops 11814043648 | bytes 21495808 | tf_op jit(solution)/shard_map/dot_general | solution.py:114
  (56 shorter events, 16.8 us)
Async XLA Ops:
  7.8 49.1 %all-to-all-start = ((s32[64,1,1]{2,1,0:T(1,128)}), s32[64,1,1]{2,1,0:T(1,128)S(1)}, u32[]{:S(2)}, u32[]{:S(2)}) async-start(s32[64,1,1]{2,1,0:T(1,128)} %broadcast_in_dim.83), calls=%async_computation | async-start | bytes 65536 | tf_op jit(solution)/shard_map/all_to_all | solution.py:15
  61.0 19.6 %all-to-all-start.2 = ((s32[64,1,1]{2,1,0:T(1,128)}), s32[64,1,1]{2,1,0:T(1,128)S(1)}, u32[]{:S(2)}, u32[]{:S(2)}) async-start(s32[64,1,1]{2,1,0:T(1,128)} %compare_select_fusion.2), calls=%async_computation.2 | async-start | bytes 65536 | tf_op jit(solution)/shard_map/all_to_all | solution.py:109
  80.6 206.5 %all-to-all-start.1 = ((bf16[64,128,512]{2,1,0:T(8,128)(2,1)}), bf16[64,128,512]{2,1,0:T(8,128)(2,1)}, u32[]{:S(2)}, u32[]{:S(2)}) async-start(bf16[64,128,512]{2,1,0:T(8,128)(2,1)} %gather_fusion), calls=%async_computation.1 | async-start | bytes 16777216 | tf_op jit(solution)/shard_map/all_to_all | solution.py:108
  89.1 203.9 %all-gather.5.cloned.1.call-start = ((), (), s32[]{:S(2)}) async-start(), calls=%async_computation.4 | async-start | bytes 4259840 | tf_op jit(solution)/shard_map/all_gather | solution.py:91
  89.8 311.9 %all-gather.3.cloned.1.call-start = ((), (), s32[]{:S(2)}) async-start(), calls=%async_computation.3 | async-start | bytes 14417920 | tf_op jit(solution)/shard_map/all_gather | solution.py:115
Sparse Core Ops, SparseCore 0:
  92.7 101.4 all-gather.4
  293.1 108.6 all-gather.2
where the time goes:
time: 427 us; the launch traced here: 426 us
  waiting for transfers between devices  307 us (72%)
  matrix products  32.6 us (8%)
  starting transfers between devices  32.2 us (8%)
  local copies, waits for them, and re-layouts  28.3 us (7%)
  between operations  14.1 us (3%)
  other arithmetic  11.8 us (3%)
    all_to_all x1, waiting for transfers between devices, body(): lax.all_to_all(own_result[chosen], 'dp', split_axis=0, concat_axis=0, til...  196 us
    all_gather x1, waiting for transfers between devices, body(): lax.all_gather(flattened, 'mp', axis=1, tiled=True)  109 us
    dot_general x1, matrix products, body(): jnp.dot(lax.all_gather(flattened, 'mp', axis=1, tiled=True), full_weight,...  17.8 us
    all_to_all x1, starting transfers between devices, from_everyone(): lax.all_to_all(jnp.broadcast_to(shard[None], (size, *shard.shape)), axis,...  13.1 us
    all_to_all x1, starting transfers between devices, body(): lax.all_to_all(labels, 'dp', split_axis=0, concat_axis=0, tiled=True)  10.3 us
  transfers between devices with their start and end apart: 5, of which 3 were waited for; matrix products, arithmetic and copies ran while one was open for 12% of the time, Pallas kernels for 0%

commit v1 on v0

--- a/solution.py
+++ b/solution.py
@@ -112,7 +112,15 @@
     attended = arrived[0][source]
     flattened = attended.reshape(kept_blocks * BLOCK, query_cols)
     mixed = jnp.dot(
-        lax.all_gather(flattened, "mp", axis=1, tiled=True),
+        jnp.concatenate(
+            lax.all_to_all(
+                jnp.stack([flattened for _ in range(lax.psum(1, "mp"))]),
+                "mp",
+                split_axis=0,
+                concat_axis=0,
+            ),
+            axis=1,
+        ),
         full_weight,
         preferred_element_type=jnp.float32,
     )

time: 427 us -> 449 us (1.052)
  local copies, waits for them, and re-layouts: 28.3 us -> 36.2 us
  starting transfers between devices: 32.2 us -> 39 us
  waiting for transfers between devices: 307 us -> 313 us
    all_gather x1 -> x0, waiting for transfers between devices: 109 us -> none  [body(): lax.all_gather(flattened, 'mp', axis=1, tiled=True)]
    all_gather x1, waiting for transfers between devices: 0.02 us -> 79.1 us  [body(): full_weight = lax.all_gather(out_weight, 'dp', axis=0, tiled=True)]
    all_to_all x0 -> x1, waiting for transfers between devices: none -> 48.2 us  [body(): lax.all_to_all(jnp.stack([flattened for _ in range(lax.psum(1, 'mp'))]),...]
    all_to_all x1, waiting for transfers between devices: 196 us -> 184 us  [body(): lax.all_to_all(own_result[chosen], 'dp', split_axis=0, concat_axis=0, til...]
    another operation x0 -> x2, local copies, waits for them, and re-layouts: none -> 8.08 us  [body(): jnp.stack([flattened for _ in range(lax.psum(1, 'mp'))])]
    all_to_all x0 -> x1, starting transfers between devices: none -> 6.15 us  [body(): lax.all_to_all(jnp.stack([flattened for _ in range(lax.psum(1, 'mp'))]),...]
  transfers between devices with their start and end apart: 5 -> 5, of which waited for: 3 -> 4; matrix products, arithmetic and copies ran while one was open for 12% -> 10% of each run, Pallas kernels for 0% -> 0%
where the time goes in v1:
time: 449 us; the launch traced here: 447 us
  waiting for transfers between devices  313 us (70%)
  starting transfers between devices  39 us (9%)
  local copies, waits for them, and re-layouts  36.2 us (8%)
  matrix products  32.7 us (7%)
  between operations  14.1 us (3%)
  other arithmetic  11.8 us (3%)
    all_to_all x1, waiting for transfers between devices, body(): lax.all_to_all(own_result[chosen], 'dp', split_axis=0, concat_axis=0, til...  184 us
    all_gather x1, waiting for transfers between devices, body(): full_weight = lax.all_gather(out_weight, 'dp', axis=0, tiled=True)  79.1 us
    all_to_all x1, waiting for transfers between devices, body(): lax.all_to_all(jnp.stack([flattened for _ in range(lax.psum(1, 'mp'))]),...  48.2 us
    dot_general x1, matrix products, body(): jnp.dot(jnp.concatenate(lax.all_to_all(jnp.stack([flattened for _ in rang...  17.9 us
    all_to_all x1, starting transfers between devices, from_everyone(): lax.all_to_all(jnp.broadcast_to(shard[None], (size, *shard.shape)), axis,...  13.1 us
    all_to_all x1, starting transfers between devices, body(): lax.all_to_all(labels, 'dp', split_axis=0, concat_axis=0, tiled=True)  10.3 us
    all_to_all x1, starting transfers between devices, body(): lax.all_to_all(own_result[chosen], 'dp', split_axis=0, concat_axis=0, til...  9.17 us
  transfers between devices with their start and end apart: 5, of which 4 were waited for; matrix products, arithmetic and copies ran while one was open for 10% of the time, Pallas kernels for 0%

profile of v1, /device:TPU:1, one launch (start us, length us, event | category | flops | bytes accessed | tf_op | source)
XLA Modules:
  0.0 447.5 jit_solution(9015103677063134631)
XLA Ops:
  7.8 13.1 %all-to-all-start = ((s32[64,1,1]{2,1,0:T(1,128)}), s32[64,1,1]{2,1,0:T(1,128)S(1)}, u32[]{:S(2)}, u32[]{:S(2)}) async-start(s32[64,1,1]{2,1,0:T(1,128)} %broadcast_in_dim.83), calls=%async_computation | async-start | bytes 65536 | tf_op jit(solution)/shard_map/all_to_all | solution.py:15
  21.0 35.8 %while.10 = (s32[]{:T(128)}, bf16[6,4,128,512]{3,2,1,0:T(8,128)(2,1)}, s32[6,4,128]{2,1,0:T(4,128)}, bf16[6,4,128,128]{3,2,1,0:T(8,128)(2,1)}, bf16[6,4,128,128]...) while((s32[]{:T(128)}, bf16[6,4,128,512]{3,2,1,0:T(8,128)(2,1)}, s32[6,4,128]{2,1,0:T(4,128)}, ...), condition=%wide.region_3.4_spmd, body=%wide.region_0.3_spmd.sunk | while | flops 137507328 | bytes 8995413 | solution.py:72
  21.8 1.1 constant_dynamic-slice_fusion.2
  23.2 1.2 fusion.33
  24.6 1.3 select_convert_fusion.2
  27.8 1.1 constant_dynamic-slice_fusion.2
  29.2 1.2 fusion.33
  30.6 1.3 select_convert_fusion.2
  33.7 1.1 constant_dynamic-slice_fusion.2
  35.1 1.2 fusion.33
  36.5 1.3 select_convert_fusion.2
  41.1 1.2 fusion.33
  42.5 1.3 select_convert_fusion.2
  47.0 1.2 fusion.33
  48.5 1.3 select_convert_fusion.2
  53.0 1.2 fusion.33
  54.4 1.3 select_convert_fusion.2
  56.7 1.2 reduce.2
  58.7 1.4 compare_select_fusion.2
  60.1 10.3 %all-to-all-start.2 = ((s32[64,1,1]{2,1,0:T(1,128)}), s32[64,1,1]{2,1,0:T(1,128)S(1)}, u32[]{:S(2)}, u32[]{:S(2)}) async-start(s32[64,1,1]{2,1,0:T(1,128)} %compare_select_fusion.2), calls=%async_computation.2 | async-start | bytes 65536 | tf_op jit(solution)/shard_map/all_to_all | solution.py:109
  71.2 7.3 %gather_fusion = bf16[64,128,512]{2,1,0:T(8,128)(2,1)} fusion(bf16[24,128,512]{2,1,0:T(8,128)(2,1)} %bitcast.79, s32[1024]{0:T(1024)S(1)} %pad_clamp_fusion.1), kind=kCustom, calls=%fused_computation | custom fusion | bytes 16777472 | tf_op jit(solution)/shard_map/gather | solution.py:108
  78.5 1.2 all-to-all-done.2
  79.7 9.2 %all-to-all-start.1 = ((bf16[64,128,512]{2,1,0:T(8,128)(2,1)}), bf16[64,128,512]{2,1,0:T(8,128)(2,1)}, u32[]{:S(2)}, u32[]{:S(2)}) async-start(bf16[64,128,512]{2,1,0:T(8,128)(2,1)} %gather_fusion), calls=%async_computation.1 | async-start | bytes 16777216 | tf_op jit(solution)/shard_map/all_to_all | solution.py:108
  88.9 1.2 reduce.3
  90.4 184.3 %all-to-all-done.1 = bf16[64,128,512]{2,1,0:T(8,128)(2,1)} async-done(((bf16[64,128,512]{2,1,0:T(8,128)(2,1)}), bf16[64,128,512]{2,1,0:T(8,128)(2,1)}, u32[]{:S(2)}, u32[]{:S(2)}) %all-to-all-start.1) | async-done | bytes 8388640 | tf_op jit(solution)/shard_map/all_to_all | solution.py:108
  274.7 5.8 %gather_fusion.1 = bf16[22,128,512]{2,1,0:T(8,128)(2,1)} fusion(bf16[64,128,512]{2,1,0:T(8,128)(2,1)} %all-to-all-done.1, s32[1024]{0:T(1024)S(1)} %pad_clamp_fusion), kind=kCustom, calls=%fused_computation.1 | custom fusion | bytes 5767256 | tf_op jit(solution)/shard_map/gather | solution.py:112
  280.5 3.1 copy.40
  283.6 5.0 %stack.3 = bf16[4,2816,512]{1,2,0:T(8,128)(2,1)} broadcast(bf16[2816,512]{0,1:T(8,128)(2,1)S(1)} %copy.40), dimensions={1,2} | broadcast | bytes 14417920 | tf_op jit(solution)/shard_map/stack | solution.py:117
  288.6 6.2 %all-to-all-start.3 = ((bf16[4,2816,512]{1,2,0:T(8,128)(2,1)}), bf16[4,2816,512]{1,2,0:T(8,128)(2,1)}, u32[]{:S(2)}, u32[]{:S(2)}) async-start(bf16[4,2816,512]{1,2,0:T(8,128)(2,1)} %stack.3), calls=%async_computation.3 | async-start | bytes 23068672 | tf_op jit(solution)/shard_map/all_to_all | solution.py:116
  295.5 79.1 %all-gather.2.cloned.1.call-done = bf16[2048,1024]{1,0:T(8,128)(2,1)} async-done(((bf16[32,1024]{1,0:T(8,128)(2,1)}), bf16[2048,1024]{1,0:T(8,128)(2,1)}) %all-gather.2.cloned.1.call-update) | async-done | bytes 4194320 | tf_op jit(solution)/shard_map/all_gather | solution.py:91
  374.6 48.2 %all-to-all-done.3 = bf16[4,2816,512]{1,2,0:T(8,128)(2,1)} async-done(((bf16[4,2816,512]{1,2,0:T(8,128)(2,1)}), bf16[4,2816,512]{1,2,0:T(8,128)(2,1)}, u32[]{:S(2)}, u32[]{:S(2)}) %all-to-all-start.3) | async-done | bytes 11534368 | tf_op jit(solution)/shard_map/all_to_all | solution.py:116
  422.8 17.9 %convolution_convert_fusion = bf16[2816,1024]{1,0:T(8,128)(2,1)} fusion(bf16[2816,2048]{0,1:T(8,128)(2,1)} %bitcast.28, bf16[2048,1024]{1,0:T(8,128)(2,1)} %all-gather.2.cloned.1.call-done), kind=kOutput, calls=%fused_computation.27 | convolution fusion | flops 11814043648 | bytes 21495808 | tf_op jit(solution)/shard_map/dot_general | solution.py:114
  (57 shorter events, 20.4 us)
Async XLA Ops:
  7.8 48.9 %all-to-all-start = ((s32[64,1,1]{2,1,0:T(1,128)}), s32[64,1,1]{2,1,0:T(1,128)S(1)}, u32[]{:S(2)}, u32[]{:S(2)}) async-start(s32[64,1,1]{2,1,0:T(1,128)} %broadcast_in_dim.83), calls=%async_computation | async-start | bytes 65536 | tf_op jit(solution)/shard_map/all_to_all | solution.py:15
  60.1 19.6 %all-to-all-start.2 = ((s32[64,1,1]{2,1,0:T(1,128)}), s32[64,1,1]{2,1,0:T(1,128)S(1)}, u32[]{:S(2)}, u32[]{:S(2)}) async-start(s32[64,1,1]{2,1,0:T(1,128)} %compare_select_fusion.2), calls=%async_computation.2 | async-start | bytes 65536 | tf_op jit(solution)/shard_map/all_to_all | solution.py:109
  79.7 194.9 %all-to-all-start.1 = ((bf16[64,128,512]{2,1,0:T(8,128)(2,1)}), bf16[64,128,512]{2,1,0:T(8,128)(2,1)}, u32[]{:S(2)}, u32[]{:S(2)}) async-start(bf16[64,128,512]{2,1,0:T(8,128)(2,1)} %gather_fusion), calls=%async_computation.1 | async-start | bytes 16777216 | tf_op jit(solution)/shard_map/all_to_all | solution.py:108
  288.6 134.2 %all-to-all-start.3 = ((bf16[4,2816,512]{1,2,0:T(8,128)(2,1)}), bf16[4,2816,512]{1,2,0:T(8,128)(2,1)}, u32[]{:S(2)}, u32[]{:S(2)}) async-start(bf16[4,2816,512]{1,2,0:T(8,128)(2,1)} %stack.3), calls=%async_computation.3 | async-start | bytes 23068672 | tf_op jit(solution)/shard_map/all_to_all | solution.py:116
  294.7 79.9 %all-gather.2.cloned.1.call-start = ((), (), s32[]{:S(2)}) async-start(), calls=%async_computation.4 | async-start | bytes 4259840 | tf_op jit(solution)/shard_map/all_gather | solution.py:91
Sparse Core Ops, SparseCore 0:
  298.3 76.2 all-gather.1
